TPU v7x, 32 devices: a whole 2x2x4 slice. The times are simulated.
32 devices in a mesh: dp: 16 (over z, y, core), group: 2 (over x).
Axes of the slice: x: 2, y: 2, z: 4, core: 2. Of those that a mesh axis runs over, the one named last changes fastest.
Arguments:
- rewards: float32 [512, 4096], P(('dp', 'group')), may hold values from -6 to 6
- values: float32 [512, 4096], P(('dp', 'group')), may hold values from -6 to 6
- horizon: float32 [512], P(('dp', 'group')), may hold values from 16 to 32768
- lengths: int32 [512], P(('dp', 'group')), may hold values from 1 to 4096
- assignment: int32 [16, 1024], P('dp', 'group'), may hold values from 0 to 1023, as said below
Outputs:
- returns: float32 [512, 4096], P(('dp', 'group'))
- train_adv: float32 [16384, 128], P(('dp', 'group'))
Inputs may be any that keep to these rules, and one draw needn't show every extreme that they name: Each row of assignment names each of the 1024 blocks of its index of dp once; the slots held by one device take at most 512 blocks from the sequences of any one device of its group, and that most is reached in every row.
All inputs are finite; a program needn't handle non-finite values.
Results may differ from a plain program's by a relative error of at most 0.0001.
Values sent between devices are 32-bit elements; how exact they have to be, the bound alone decides.
No kernel may reach another device: no remote copies, remote signals or barrier semaphores. Data moves between devices by JAX's collectives and lax.ppermute only.
A program may use at most 64 MiB of HBM per device.

v0:
```python
import functools

import jax
import jax.numpy as jnp
from jax import lax
from jax.experimental import pallas as pl
from jax.experimental.pallas import tpu as pltpu
from jax.sharding import PartitionSpec as P


BLK = 128
trace_decay = 0.998
epsilon = 1e-05
OUTSIDE = 1e30
ROWS = 8


def column(ref, first, dtype):
    row = lax.broadcasted_iota(jnp.int32, (ROWS, BLK), 0)
    out = jnp.zeros((ROWS, BLK), dtype)
    for k in range(ROWS):
        out = jnp.where(row == k, ref[first + k], out)
    return out[:, :1]


def advantage_kernel(
    horizon_hbm, lengths_hbm, rewards_hbm, values_hbm,
    returns_ref, blocks_ref, moments_ref,
    horizon_ref, lengths_ref, rewards_ref, values_ref, sems,
):
    seqs, local = rewards_ref.shape
    per_row = local // BLK
    small = [
        pltpu.make_async_copy(horizon_hbm, horizon_ref, sems.at[0]),
        pltpu.make_async_copy(lengths_hbm, lengths_ref, sems.at[1]),
    ]
    large = []
    for k in range(seqs // ROWS):
        rows = pl.ds(k * ROWS, ROWS)
        large.append(pltpu.make_async_copy(values_hbm.at[rows, :], values_ref.at[rows, :], sems.at[2 + 2 * k]))
        large.append(pltpu.make_async_copy(rewards_hbm.at[rows, :], rewards_ref.at[rows, :], sems.at[3 + 2 * k]))
    for copy in small + large:
        copy.start()
    for copy in small:
        copy.wait()
    lane = lax.broadcasted_iota(jnp.int32, (ROWS, BLK), 1)
    count = 0
    for k in range(seqs):
        count = count + lengths_ref[k]
    count = jnp.full((1, 1), count.astype(jnp.float32), jnp.float32)
    sums = jnp.zeros((ROWS, BLK), jnp.float32)
    for first in range(0, seqs, ROWS):
        rows = pl.ds(first, ROWS)
        length = column(lengths_ref, first, jnp.int32)
        discount = 1.0 - 1.0 / column(horizon_ref, first, jnp.float32)
        power = discount * trace_decay
        decay = power
        steps, step = [], 1
        while step < BLK:
            steps.append(jnp.where(lane < BLK - step, power, 0.0))
            decay = jnp.where((BLK - 1 - lane) & step != 0, decay * power, decay)
            power = power * power
            step *= 2
        for copy in large[first // ROWS * 2 : first // ROWS * 2 + 2]:
            copy.wait()
        carry = jnp.zeros((ROWS, BLK), jnp.float32)
        after = None
        for block in reversed(range(per_row)):
            at = pl.ds(block * BLK, BLK)
            rewards = rewards_ref[rows, at]
            values = values_ref[rows, at]
            inside = lane < length - block * BLK
            follows = lane + 1 < length - block * BLK
            rolled = pltpu.roll(values, BLK - 1, 1)
            after = rolled if after is None else after
            upcoming = jnp.where(follows, jnp.where(lane < BLK - 1, rolled, after), 0.0)
            after = rolled
            total = jnp.where(inside, rewards + discount * upcoming - values, 0.0)
            for k, weight in enumerate(steps):
                total = total + weight * pltpu.roll(total, BLK - 2**k, 1)
            head = jnp.broadcast_to(total[:, :1], (ROWS, BLK))
            total = total + decay * carry
            carry = head + power * carry
            total = jnp.where(inside, total, 0.0)
            sums = sums + total
            returns_ref[rows, at] = jnp.where(inside, total + values, 0.0)
            blocks_ref[pl.ds(first * per_row + block, ROWS, stride=per_row), :] = jnp.where(inside, total, OUTSIDE)
    mean = jnp.sum(jnp.sum(sums, axis=0, keepdims=True), axis=1, keepdims=True) / count
    squares = jnp.zeros((ROWS, BLK), jnp.float32)
    for k in range(0, blocks_ref.shape[0], ROWS):
        marked = blocks_ref[pl.ds(k, ROWS), :]
        off = jnp.where(marked == OUTSIDE, 0.0, marked - mean)
        squares = squares + off * off
    spread = jnp.sum(jnp.sum(squares, axis=0, keepdims=True), axis=1, keepdims=True)
    row = jnp.where(lane == 0, count, jnp.where(lane == 1, mean, jnp.where(lane == 2, spread, 0.0)))
    for k in range(0, moments_ref.shape[0], ROWS):
        moments_ref[pl.ds(k, ROWS), :] = row


def gather_kernel(members, wanted_hbm, returns_ref, *refs):
    sources, (moved_ref, returns_hbm, pool_ref, wanted_ref, sems) = refs[:members], refs[members:]
    slots = moved_ref.shape[0]
    share = sources[0].shape[0]
    fetch = pltpu.make_async_copy(wanted_hbm, wanted_ref, sems.at[0])
    fetch.start()
    write = pltpu.make_async_copy(returns_ref, returns_hbm, sems.at[1])
    write.start()
    group = lax.axis_index("group")
    for k in range(members):
        owner = lax.rem(group + k, members)
        pool_ref[pl.ds(pl.multiple_of(owner * share, share), share), :] = sources[k][...]
    fetch.wait()

    def move(i, carry):
        first = pl.multiple_of(i * ROWS, ROWS)
        for k in range(ROWS):
            moved_ref[pl.ds(first + k, 1), :] = pool_ref[pl.ds(wanted_ref[0, first + k], 1), :]
        return carry

    lax.fori_loop(0, slots // ROWS, move, 0)
    write.wait()


def whiten_kernel(moments_ref, moved_ref, train_hbm, train_ref, sems):
    moments = moments_ref[...]
    count, mean, spread = moments[:, 0:1], moments[:, 1:2], moments[:, 2:3]
    total = jnp.sum(count, axis=0, keepdims=True)
    center = jnp.sum(count * mean, axis=0, keepdims=True) / total
    deviation = jnp.sum(spread + count * (mean - center) ** 2, axis=0, keepdims=True)
    scale = jnp.broadcast_to(lax.rsqrt(deviation / total + epsilon), (1, BLK))
    center = jnp.broadcast_to(center, (1, BLK))
    pieces = sems.shape[0]
    depth = moved_ref.shape[0] // pieces
    copies = []
    for k in range(pieces):
        rows = pl.ds(k * depth, depth)
        moved = moved_ref[rows, :]
        train_ref[rows, :] = jnp.where(moved == OUTSIDE, 0.0, (moved - center) * scale)
        copies.append(pltpu.make_async_copy(train_ref.at[rows, :], train_hbm.at[rows, :], sems.at[k]))
        copies[-1].start()
    for copy in copies:
        copy.wait()


def in_hbm(array):
    return pltpu.with_memory_space_constraint(array, pltpu.HBM)


def body(rewards, values, horizon, lengths, assignment):
    seqs, local = rewards.shape
    n_dp, n_group = lax.axis_size("dp"), lax.axis_size("group")
    slots = assignment.shape[-1]
    vmem = pl.BlockSpec(memory_space=pltpu.VMEM)
    hbm = pl.BlockSpec(memory_space=pltpu.HBM)
    params = pltpu.CompilerParams(vmem_limit_bytes=16 << 20)
    f32, i32 = jnp.float32, jnp.int32
    share = seqs * local // BLK
    returns, blocks, moments = pl.pallas_call(
        advantage_kernel,
        out_shape=(
            jax.ShapeDtypeStruct((seqs, local), f32),
            jax.ShapeDtypeStruct((share, BLK), f32),
            jax.ShapeDtypeStruct((n_dp * n_group, BLK), f32),
        ),
        in_specs=[hbm, hbm, hbm, hbm],
        out_specs=(vmem, vmem, vmem),
        scratch_shapes=[
            pltpu.SMEM((seqs,), f32),
            pltpu.SMEM((seqs,), i32),
            pltpu.VMEM((seqs, local), f32),
            pltpu.VMEM((seqs, local), f32),
            pltpu.SemaphoreType.DMA((2 + 2 * (seqs // ROWS),)),
        ],
        compiler_params=params,
        name="advantage",
    )(*map(in_hbm, (horizon, lengths, rewards, values)))
    sources = [blocks]
    for k in range(1, n_group):
        sources.append(lax.ppermute(blocks, "group", [((i + k) % n_group, i) for i in range(n_group)]))
    moments = lax.all_to_all(moments, ("dp", "group"), 0, 0, tiled=True)
    moved, returns = pl.pallas_call(
        functools.partial(gather_kernel, n_group),
        out_shape=(jax.ShapeDtypeStruct((slots, BLK), f32), jax.ShapeDtypeStruct((seqs, local), f32)),
        in_specs=[hbm, vmem] + [vmem] * n_group,
        out_specs=(vmem, hbm),
        scratch_shapes=[
            pltpu.VMEM((n_group * share, BLK), f32),
            pltpu.SMEM((1, slots), i32),
            pltpu.SemaphoreType.DMA((2,)),
        ],
        compiler_params=params,
        name="gather",
    )(in_hbm(assignment), returns, *sources)
    train = pl.pallas_call(
        whiten_kernel,
        out_shape=jax.ShapeDtypeStruct((slots, BLK), f32),
        in_specs=[vmem, vmem],
        out_specs=hbm,
        scratch_shapes=[pltpu.VMEM((slots, BLK), f32), pltpu.SemaphoreType.DMA((4,))],
        compiler_params=params,
        name="whiten",
    )(moments, moved)
    return (returns, train)


def solution(mesh):
    in_specs = (
        P(("dp", "group"), None),
        P(("dp", "group"), None),
        P(("dp", "group")),
        P(("dp", "group")),
        P("dp", "group"),
    )
    out_specs = (P(("dp", "group"), None), P(("dp", "group"), None))

    return jax.shard_map(body, mesh=mesh, in_specs=in_specs, out_specs=out_specs, check_vma=False)
```

profile of v0, /device:TPU:0, one launch (start us, length us, event | category | flops | bytes accessed | tf_op | source)
XLA Modules:
  0.0 20.2 jit_solution(7232948459083905979)
XLA Ops:
  0.6 3.3 %advantage.1 = (f32[16,4096]{1,0:T(8,128)S(1)}, f32[512,128]{1,0:T(8,128)S(1)}, f32[32,128]{1,0:T(8,128)}) custom-call(f32[16]{0:T(128)} %horizon_hbm.1, s32[16]{0:T(128)} %lengths_hbm.1, f32[16,4096]{1,0:T(8,128)} %rewards_hbm.1, f32[16,4096]{1,0:T(8,128)} %values_hbm.1), custom_call_target="tpu_custom_call" | custom-call | tf_op jit(solution)/shard_map/advantage/pallas_call | solution.py:158
  4.0 3.0 %collective-permute-start = (f32[512,128]{1,0:T(8,128)S(1)}, f32[512,128]{1,0:T(8,128)S(1)}, u32[]{:S(2)}, u32[]{:S(2)}) collective-permute-start(f32[512,128]{1,0:T(8,128)S(1)} %get-tuple-element.8.refs_0_), channel_id=1, source_target_pairs={{1,0},{0,1},{3,2},{2,3},{5,4},{4,5},{7,6},{6,7},{9,8},{8,9},{11,10... | collective-permute-start | bytes 786440 | tf_op jit(solution)/shard_map/ppermute | solution.py:179
  7.0 4.9 %all-to-all-start = ((f32[32,1,128]{2,1,0:T(1,128)}), f32[32,1,128]{2,1,0:T(1,128)S(1)}, u32[]{:S(2)}, u32[]{:S(2)}) async-start(f32[32,1,128]{2,1,0:T(1,128)} %bitcast.1), calls=%async_computation | async-start | bytes 32768 | tf_op jit(solution)/shard_map/all_to_all | solution.py:180
  11.9 1.4 %collective-permute-done.refs_1_ = f32[512,128]{1,0:T(8,128)S(1)} collective-permute-done((f32[512,128]{1,0:T(8,128)S(1)}, f32[512,128]{1,0:T(8,128)S(1)}, u32[]{:S(2)}, u32[]{:S(2)}) %collective-permute-start) | collective-permute-done | bytes 262176 | tf_op jit(solution)/shard_map/ppermute | solution.py:179
  13.3 1.3 %gather.1 = (f32[512,128]{1,0:T(8,128)S(1)}, f32[16,4096]{1,0:T(8,128)}) custom-call(s32[1,512]{1,0:T(1,128)} %wanted_hbm.1, f32[16,4096]{1,0:T(8,128)S(1)} %get-tuple-element.7.returns_ref, f32[512,128]{1,0:T(8,128)S(1)} %get-tuple-element.8.refs_0_, f32[512,128]{1,0:T(8,128)S(1)} %collective-permute-done.refs_1_), custom_call_target="tpu_custom_call" | custom-call | tf_op jit(solution)/shard_map/gather/pallas_call | solution.py:181
  14.7 4.4 %all-to-all-done = f32[32,1,128]{2,1,0:T(1,128)S(1)} async-done(((f32[32,1,128]{2,1,0:T(1,128)}), f32[32,1,128]{2,1,0:T(1,128)S(1)}, u32[]{:S(2)}, u32[]{:S(2)}) %all-to-all-start) | async-done | bytes 16416 | tf_op jit(solution)/shard_map/all_to_all | solution.py:180
  19.1 1.1 %whiten.1 = f32[512,128]{1,0:T(8,128)} custom-call(f32[32,128]{1,0:T(8,128)S(1)} %bitcast.4, f32[512,128]{1,0:T(8,128)S(1)} %get-tuple-element.11.moved_ref), custom_call_target="tpu_custom_call" | custom-call | tf_op jit(solution)/shard_map/whiten/pallas_call | solution.py:194
Async XLA Ops:
  4.0 9.3 %collective-permute-start = (f32[512,128]{1,0:T(8,128)S(1)}, f32[512,128]{1,0:T(8,128)S(1)}, u32[]{:S(2)}, u32[]{:S(2)}) collective-permute-start(f32[512,128]{1,0:T(8,128)S(1)} %get-tuple-element.8.refs_0_), channel_id=1, source_target_pairs={{1,0},{0,1},{3,2},{2,3},{5,4},{4,5},{7,6},{6,7},{9,8},{8,9},{11,10... | collective-permute-start | bytes 786440 | tf_op jit(solution)/shard_map/ppermute | solution.py:179
  7.0 12.1 %all-to-all-start = ((f32[32,1,128]{2,1,0:T(1,128)}), f32[32,1,128]{2,1,0:T(1,128)S(1)}, u32[]{:S(2)}, u32[]{:S(2)}) async-start(f32[32,1,128]{2,1,0:T(1,128)} %bitcast.1), calls=%async_computation | async-start | bytes 32768 | tf_op jit(solution)/shard_map/all_to_all | solution.py:180
where the time goes:
time: 20.4 us; the launch traced here: 20.2 us
  starting transfers between devices  7.95 us (39%)
  Pallas kernels  5.83 us (29%)
  waiting for transfers between devices  5.8 us (28%)
  between operations  0.66 us (3%)
    all_to_all x1, starting transfers between devices, body(): moments = lax.all_to_all(moments, ('dp', 'group'), 0, 0, tiled=True)  4.92 us
    all_to_all x1, waiting for transfers between devices, body(): moments = lax.all_to_all(moments, ('dp', 'group'), 0, 0, tiled=True)  4.42 us
    pallas_call x1, Pallas kernels, body(): pl.pallas_call(advantage_kernel, out_shape=(jax.ShapeDtypeStruct((seqs, l...  3.34 us
    ppermute x1, starting transfers between devices, body(): lax.ppermute(blocks, 'group', [((i + k) % n_group, i) for i in range(n_gr...  3.03 us
    ppermute x1, waiting for transfers between devices, body(): lax.ppermute(blocks, 'group', [((i + k) % n_group, i) for i in range(n_gr...  1.38 us
    pallas_call x1, Pallas kernels, body(): pl.pallas_call(functools.partial(gather_kernel, n_group), out_shape=(jax....  1.35 us
    pallas_call x1, Pallas kernels, body(): pl.pallas_call(whiten_kernel, out_shape=jax.ShapeDtypeStruct((slots, BLK)...  1.14 us
  transfers between devices with their start and end apart: 2, of which 2 were waited for; matrix products, arithmetic and copies ran while one was open for 0% of the time, Pallas kernels for 7%

commit v1 on v0

--- a/solution.py
+++ b/solution.py
@@ -11,6 +11,7 @@
 BLK = 128
 trace_decay = 0.998
 epsilon = 1e-05
+VALUE_SHARE = 1.0 / trace_decay - 1.0
 OUTSIDE = 1e30
 ROWS = 8
 
@@ -48,43 +49,50 @@
     for k in range(seqs):
         count = count + lengths_ref[k]
     count = jnp.full((1, 1), count.astype(jnp.float32), jnp.float32)
+    above = lax.broadcasted_iota(jnp.int32, (BLK, 2 * BLK), 0)
+    across = lax.broadcasted_iota(jnp.int32, (BLK, 2 * BLK), 1)
+    ones = jnp.where((across >= BLK) | (above >= across), 1.0, 0.0).astype(jnp.bfloat16)
+    ones = jnp.concatenate([ones] * 3, axis=0)
     sums = jnp.zeros((ROWS, BLK), jnp.float32)
     for first in range(0, seqs, ROWS):
         rows = pl.ds(first, ROWS)
-        length = column(lengths_ref, first, jnp.int32)
-        discount = 1.0 - 1.0 / column(horizon_ref, first, jnp.float32)
-        power = discount * trace_decay
-        decay = power
-        steps, step = [], 1
+        left = column(lengths_ref, first, jnp.int32) - lane
+        power = (1.0 - 1.0 / column(horizon_ref, first, jnp.float32)) * trace_decay
+        rise, step = jnp.ones((ROWS, BLK), jnp.float32), 1
         while step < BLK:
-            steps.append(jnp.where(lane < BLK - step, power, 0.0))
-            decay = jnp.where((BLK - 1 - lane) & step != 0, decay * power, decay)
+            rise = jnp.where(lane & step != 0, rise * power, rise)
             power = power * power
             step *= 2
+        fall = 1.0 / rise
+        decay = power * fall
+        power = jnp.broadcast_to(power, (ROWS, BLK))
         for copy in large[first // ROWS * 2 : first // ROWS * 2 + 2]:
             copy.wait()
+        terms = []
+        for block in range(per_row):
+            at = pl.ds(block * BLK, BLK)
+            term = rewards_ref[rows, at] + VALUE_SHARE * values_ref[rows, at]
+            terms.append(jnp.where(left > block * BLK, term, 0.0) * rise)
+        rest = jnp.concatenate(terms, axis=0)
+        split = []
+        for k in range(3):
+            split.append(rest.astype(jnp.bfloat16))
+            if k < 2:
+                rest = rest - split[-1].astype(jnp.float32)
+        inner = jnp.dot(jnp.concatenate(split, axis=1), ones, preferred_element_type=jnp.float32)
         carry = jnp.zeros((ROWS, BLK), jnp.float32)
-        after = None
         for block in reversed(range(per_row)):
             at = pl.ds(block * BLK, BLK)
-            rewards = rewards_ref[rows, at]
+            own = slice(block * ROWS, (block + 1) * ROWS)
+            inside = left > block * BLK
+            total = inner[own, :BLK] * fall + decay * carry
+            carry = inner[own, BLK:] + power * carry
             values = values_ref[rows, at]
-            inside = lane < length - block * BLK
-            follows = lane + 1 < length - block * BLK
-            rolled = pltpu.roll(values, BLK - 1, 1)
-            after = rolled if after is None else after
-            upcoming = jnp.where(follows, jnp.where(lane < BLK - 1, rolled, after), 0.0)
-            after = rolled
-            total = jnp.where(inside, rewards + discount * upcoming - values, 0.0)
-            for k, weight in enumerate(steps):
-                total = total + weight * pltpu.roll(total, BLK - 2**k, 1)
-            head = jnp.broadcast_to(total[:, :1], (ROWS, BLK))
-            total = total + decay * carry
-            carry = head + power * carry
-            total = jnp.where(inside, total, 0.0)
-            sums = sums + total
-            returns_ref[rows, at] = jnp.where(inside, total + values, 0.0)
-            blocks_ref[pl.ds(first * per_row + block, ROWS, stride=per_row), :] = jnp.where(inside, total, OUTSIDE)
+            result = jnp.where(inside, total - VALUE_SHARE * values, 0.0)
+            returns_ref[rows, at] = result
+            advantage = result - values
+            sums = sums + jnp.where(inside, advantage, 0.0)
+            blocks_ref[pl.ds(first * per_row + block, ROWS, stride=per_row), :] = jnp.where(inside, advantage, OUTSIDE)
     mean = jnp.sum(jnp.sum(sums, axis=0, keepdims=True), axis=1, keepdims=True) / count
     squares = jnp.zeros((ROWS, BLK), jnp.float32)
     for k in range(0, blocks_ref.shape[0], ROWS):
@@ -160,7 +168,7 @@
         out_shape=(
             jax.ShapeDtypeStruct((seqs, local), f32),
             jax.ShapeDtypeStruct((share, BLK), f32),
-            jax.ShapeDtypeStruct((n_dp * n_group, BLK), f32),
+            pltpu.VMEM((n_dp * n_group, BLK), f32),
         ),
         in_specs=[hbm, hbm, hbm, hbm],
         out_specs=(vmem, vmem, vmem),

time: 20.4 us -> 19.7 us (0.966)
  Pallas kernels: 5.83 us -> 5.13 us
    pallas_call x1, Pallas kernels: 3.34 us -> 2.64 us  [body(): pl.pallas_call(advantage_kernel, out_shape=(jax.ShapeDtypeStruct((seqs, l...]
where the time goes in v1:
time: 19.7 us; the launch traced here: 19.5 us
  starting transfers between devices  7.95 us (40%)
  waiting for transfers between devices  5.8 us (29%)
  Pallas kernels  5.13 us (26%)
  between operations  0.66 us (3%)
    all_to_all x1, starting transfers between devices, body(): moments = lax.all_to_all(moments, ('dp', 'group'), 0, 0, tiled=True)  4.92 us
    all_to_all x1, waiting for transfers between devices, body(): moments = lax.all_to_all(moments, ('dp', 'group'), 0, 0, tiled=True)  4.42 us
    ppermute x1, starting transfers between devices, body(): lax.ppermute(blocks, 'group', [((i + k) % n_group, i) for i in range(n_gr...  3.03 us
    pallas_call x1, Pallas kernels, body(): pl.pallas_call(advantage_kernel, out_shape=(jax.ShapeDtypeStruct((seqs, l...  2.64 us
    ppermute x1, waiting for transfers between devices, body(): lax.ppermute(blocks, 'group', [((i + k) % n_group, i) for i in range(n_gr...  1.38 us
    pallas_call x1, Pallas kernels, body(): pl.pallas_call(functools.partial(gather_kernel, n_group), out_shape=(jax....  1.35 us
    pallas_call x1, Pallas kernels, body(): pl.pallas_call(whiten_kernel, out_shape=jax.ShapeDtypeStruct((slots, BLK)...  1.14 us
  transfers between devices with their start and end apart: 2, of which 2 were waited for; matrix products, arithmetic and copies ran while one was open for 0% of the time, Pallas kernels for 7%

profile of v1, /device:TPU:0, one launch (start us, length us, event | category | flops | bytes accessed | tf_op | source)
XLA Modules:
  0.0 19.5 jit_solution(6849594596313875244)
XLA Ops:
  0.6 2.6 %advantage.1 = (f32[16,4096]{1,0:T(8,128)S(1)}, f32[512,128]{1,0:T(8,128)S(1)}, f32[32,128]{1,0:T(8,128)}) custom-call(f32[16]{0:T(128)} %horizon_hbm.1, s32[16]{0:T(128)} %lengths_hbm.1, f32[16,4096]{1,0:T(8,128)} %rewards_hbm.1, f32[16,4096]{1,0:T(8,128)} %values_hbm.1), custom_call_target="tpu_custom_call" | custom-call | tf_op jit(solution)/shard_map/advantage/pallas_call | solution.py:166
  3.3 3.0 %collective-permute-start = (f32[512,128]{1,0:T(8,128)S(1)}, f32[512,128]{1,0:T(8,128)S(1)}, u32[]{:S(2)}, u32[]{:S(2)}) collective-permute-start(f32[512,128]{1,0:T(8,128)S(1)} %get-tuple-element.8.refs_0_), channel_id=1, source_target_pairs={{1,0},{0,1},{3,2},{2,3},{5,4},{4,5},{7,6},{6,7},{9,8},{8,9},{11,10... | collective-permute-start | bytes 786440 | tf_op jit(solution)/shard_map/ppermute | solution.py:187
  6.3 4.9 %all-to-all-start = ((f32[32,1,128]{2,1,0:T(1,128)}), f32[32,1,128]{2,1,0:T(1,128)S(1)}, u32[]{:S(2)}, u32[]{:S(2)}) async-start(f32[32,1,128]{2,1,0:T(1,128)} %bitcast.1), calls=%async_computation | async-start | bytes 32768 | tf_op jit(solution)/shard_map/all_to_all | solution.py:188
  11.2 1.4 %collective-permute-done.refs_1_ = f32[512,128]{1,0:T(8,128)S(1)} collective-permute-done((f32[512,128]{1,0:T(8,128)S(1)}, f32[512,128]{1,0:T(8,128)S(1)}, u32[]{:S(2)}, u32[]{:S(2)}) %collective-permute-start) | collective-permute-done | bytes 262176 | tf_op jit(solution)/shard_map/ppermute | solution.py:187
  12.6 1.3 %gather.1 = (f32[512,128]{1,0:T(8,128)S(1)}, f32[16,4096]{1,0:T(8,128)}) custom-call(s32[1,512]{1,0:T(1,128)} %wanted_hbm.1, f32[16,4096]{1,0:T(8,128)S(1)} %get-tuple-element.7.returns_ref, f32[512,128]{1,0:T(8,128)S(1)} %get-tuple-element.8.refs_0_, f32[512,128]{1,0:T(8,128)S(1)} %collective-permute-done.refs_1_), custom_call_target="tpu_custom_call" | custom-call | tf_op jit(solution)/shard_map/gather/pallas_call | solution.py:189
  14.0 4.4 %all-to-all-done = f32[32,1,128]{2,1,0:T(1,128)S(1)} async-done(((f32[32,1,128]{2,1,0:T(1,128)}), f32[32,1,128]{2,1,0:T(1,128)S(1)}, u32[]{:S(2)}, u32[]{:S(2)}) %all-to-all-start) | async-done | bytes 16416 | tf_op jit(solution)/shard_map/all_to_all | solution.py:188
  18.4 1.1 %whiten.1 = f32[512,128]{1,0:T(8,128)} custom-call(f32[32,128]{1,0:T(8,128)S(1)} %bitcast.4, f32[512,128]{1,0:T(8,128)S(1)} %get-tuple-element.11.moved_ref), custom_call_target="tpu_custom_call" | custom-call | tf_op jit(solution)/shard_map/whiten/pallas_call | solution.py:202
Async XLA Ops:
  3.3 9.3 %collective-permute-start = (f32[512,128]{1,0:T(8,128)S(1)}, f32[512,128]{1,0:T(8,128)S(1)}, u32[]{:S(2)}, u32[]{:S(2)}) collective-permute-start(f32[512,128]{1,0:T(8,128)S(1)} %get-tuple-element.8.refs_0_), channel_id=1, source_target_pairs={{1,0},{0,1},{3,2},{2,3},{5,4},{4,5},{7,6},{6,7},{9,8},{8,9},{11,10... | collective-permute-start | bytes 786440 | tf_op jit(solution)/shard_map/ppermute | solution.py:187
  6.3 12.1 %all-to-all-start = ((f32[32,1,128]{2,1,0:T(1,128)}), f32[32,1,128]{2,1,0:T(1,128)S(1)}, u32[]{:S(2)}, u32[]{:S(2)}) async-start(f32[32,1,128]{2,1,0:T(1,128)} %bitcast.1), calls=%async_computation | async-start | bytes 32768 | tf_op jit(solution)/shard_map/all_to_all | solution.py:188

commit v2 on v1

--- a/solution.py
+++ b/solution.py
@@ -14,6 +14,7 @@
 VALUE_SHARE = 1.0 / trace_decay - 1.0
 OUTSIDE = 1e30
 ROWS = 8
+PART = BLK // 4
 
 
 def column(ref, first, dtype):
@@ -22,6 +23,10 @@
     for k in range(ROWS):
         out = jnp.where(row == k, ref[first + k], out)
     return out[:, :1]
+
+
+def whole(tile):
+    return jnp.sum(jnp.sum(tile, axis=0, keepdims=True), axis=1, keepdims=True)
 
 
 def advantage_kernel(
@@ -35,11 +40,10 @@
         pltpu.make_async_copy(horizon_hbm, horizon_ref, sems.at[0]),
         pltpu.make_async_copy(lengths_hbm, lengths_ref, sems.at[1]),
     ]
-    large = []
-    for k in range(seqs // ROWS):
-        rows = pl.ds(k * ROWS, ROWS)
-        large.append(pltpu.make_async_copy(values_hbm.at[rows, :], values_ref.at[rows, :], sems.at[2 + 2 * k]))
-        large.append(pltpu.make_async_copy(rewards_hbm.at[rows, :], rewards_ref.at[rows, :], sems.at[3 + 2 * k]))
+    large = [
+        pltpu.make_async_copy(values_hbm, values_ref, sems.at[2]),
+        pltpu.make_async_copy(rewards_hbm, rewards_ref, sems.at[3]),
+    ]
     for copy in small + large:
         copy.start()
     for copy in small:
@@ -53,9 +57,8 @@
     across = lax.broadcasted_iota(jnp.int32, (BLK, 2 * BLK), 1)
     ones = jnp.where((across >= BLK) | (above >= across), 1.0, 0.0).astype(jnp.bfloat16)
     ones = jnp.concatenate([ones] * 3, axis=0)
-    sums = jnp.zeros((ROWS, BLK), jnp.float32)
+    groups = []
     for first in range(0, seqs, ROWS):
-        rows = pl.ds(first, ROWS)
         left = column(lengths_ref, first, jnp.int32) - lane
         power = (1.0 - 1.0 / column(horizon_ref, first, jnp.float32)) * trace_decay
         rise, step = jnp.ones((ROWS, BLK), jnp.float32), 1
@@ -63,50 +66,57 @@
             rise = jnp.where(lane & step != 0, rise * power, rise)
             power = power * power
             step *= 2
-        fall = 1.0 / rise
-        decay = power * fall
-        power = jnp.broadcast_to(power, (ROWS, BLK))
-        for copy in large[first // ROWS * 2 : first // ROWS * 2 + 2]:
-            copy.wait()
-        terms = []
+        groups.append((left, rise, 1.0 / rise, jnp.broadcast_to(power, (ROWS, BLK))))
+    for copy in large:
+        copy.wait()
+    terms = []
+    for g, (left, rise, _, _) in enumerate(groups):
+        rows = pl.ds(g * ROWS, ROWS)
         for block in range(per_row):
             at = pl.ds(block * BLK, BLK)
             term = rewards_ref[rows, at] + VALUE_SHARE * values_ref[rows, at]
             terms.append(jnp.where(left > block * BLK, term, 0.0) * rise)
-        rest = jnp.concatenate(terms, axis=0)
-        split = []
-        for k in range(3):
-            split.append(rest.astype(jnp.bfloat16))
-            if k < 2:
-                rest = rest - split[-1].astype(jnp.float32)
-        inner = jnp.dot(jnp.concatenate(split, axis=1), ones, preferred_element_type=jnp.float32)
-        carry = jnp.zeros((ROWS, BLK), jnp.float32)
+    rest = jnp.concatenate(terms, axis=0)
+    split = []
+    for k in range(3):
+        split.append(rest.astype(jnp.bfloat16))
+        if k < 2:
+            rest = rest - split[-1].astype(jnp.float32)
+    inner = jnp.dot(jnp.concatenate(split, axis=1), ones, preferred_element_type=jnp.float32)
+    moments = []
+    for g, (left, _, fall, power) in enumerate(groups):
+        rows = pl.ds(g * ROWS, ROWS)
+        carry = sums = jnp.zeros((ROWS, BLK), jnp.float32)
         for block in reversed(range(per_row)):
             at = pl.ds(block * BLK, BLK)
-            own = slice(block * ROWS, (block + 1) * ROWS)
+            tile = (g * per_row + block) * ROWS
             inside = left > block * BLK
-            total = inner[own, :BLK] * fall + decay * carry
-            carry = inner[own, BLK:] + power * carry
-            values = values_ref[rows, at]
-            result = jnp.where(inside, total - VALUE_SHARE * values, 0.0)
+            values = jnp.where(inside, values_ref[rows, at], 0.0)
+            result = fall * (inner[tile : tile + ROWS, :BLK] + carry) - VALUE_SHARE * values
+            advantage = result - values
+            carry = power * (inner[tile : tile + ROWS, BLK:] + carry)
+            sums = sums + advantage
             returns_ref[rows, at] = result
-            advantage = result - values
-            sums = sums + jnp.where(inside, advantage, 0.0)
-            blocks_ref[pl.ds(first * per_row + block, ROWS, stride=per_row), :] = jnp.where(inside, advantage, OUTSIDE)
-    mean = jnp.sum(jnp.sum(sums, axis=0, keepdims=True), axis=1, keepdims=True) / count
-    squares = jnp.zeros((ROWS, BLK), jnp.float32)
-    for k in range(0, blocks_ref.shape[0], ROWS):
-        marked = blocks_ref[pl.ds(k, ROWS), :]
-        off = jnp.where(marked == OUTSIDE, 0.0, marked - mean)
-        squares = squares + off * off
-    spread = jnp.sum(jnp.sum(squares, axis=0, keepdims=True), axis=1, keepdims=True)
-    row = jnp.where(lane == 0, count, jnp.where(lane == 1, mean, jnp.where(lane == 2, spread, 0.0)))
+            blocks_ref[pl.ds(tile, ROWS), :] = jnp.where(inside, advantage, OUTSIDE)
+        inside = lax.div(jnp.maximum(left, 0) + BLK - 1, BLK).astype(jnp.float32)
+        moments.append([inside, sums, sums / jnp.maximum(inside, 1.0)])
+    squares = []
+    for g, (_, _, middle) in enumerate(moments):
+        parts = [jnp.zeros((ROWS, BLK), jnp.float32)] * 4
+        for block in range(per_row):
+            marked = blocks_ref[pl.ds((g * per_row + block) * ROWS, ROWS), :]
+            off = jnp.where(marked == OUTSIDE, 0.0, marked - middle)
+            parts = parts[1:] + [parts[0] + off * off]
+        squares.append(sum(parts[1:], parts[0]))
+    mean = whole(sum(part[1] for part in moments)) / count
+    spread = whole(sum(square + part[0] * (part[2] - mean) ** 2 for square, part in zip(squares, moments)))
+    row = jnp.where(lane < PART, count, jnp.where(lane < 2 * PART, count * mean, jnp.where(lane < 3 * PART, mean, spread)))
     for k in range(0, moments_ref.shape[0], ROWS):
         moments_ref[pl.ds(k, ROWS), :] = row
 
 
-def gather_kernel(members, wanted_hbm, returns_ref, *refs):
-    sources, (moved_ref, returns_hbm, pool_ref, wanted_ref, sems) = refs[:members], refs[members:]
+def gather_kernel(members, per_row, wanted_hbm, returns_ref, *refs):
+    sources, (moved_ref, returns_hbm, pool_ref, wanted_ref, place_ref, sems) = refs[:members], refs[members:]
     slots = moved_ref.shape[0]
     share = sources[0].shape[0]
     fetch = pltpu.make_async_copy(wanted_hbm, wanted_ref, sems.at[0])
@@ -118,11 +128,17 @@
         owner = lax.rem(group + k, members)
         pool_ref[pl.ds(pl.multiple_of(owner * share, share), share), :] = sources[k][...]
     fetch.wait()
+    wanted = wanted_ref[...]
+    sequence, block = lax.div(wanted, per_row), lax.rem(wanted, per_row)
+    wanted_ref[...] = (lax.div(sequence, ROWS) * per_row + block) * ROWS + lax.rem(sequence, ROWS)
+    place = pltpu.make_async_copy(wanted_ref, place_ref, sems.at[0])
+    place.start()
+    place.wait()
 
     def move(i, carry):
         first = pl.multiple_of(i * ROWS, ROWS)
         for k in range(ROWS):
-            moved_ref[pl.ds(first + k, 1), :] = pool_ref[pl.ds(wanted_ref[0, first + k], 1), :]
+            moved_ref[pl.ds(first + k, 1), :] = pool_ref[pl.ds(place_ref[0, first + k], 1), :]
         return carry
 
     lax.fori_loop(0, slots // ROWS, move, 0)
@@ -131,12 +147,13 @@
 
 def whiten_kernel(moments_ref, moved_ref, train_hbm, train_ref, sems):
     moments = moments_ref[...]
-    count, mean, spread = moments[:, 0:1], moments[:, 1:2], moments[:, 2:3]
-    total = jnp.sum(count, axis=0, keepdims=True)
-    center = jnp.sum(count * mean, axis=0, keepdims=True) / total
-    deviation = jnp.sum(spread + count * (mean - center) ** 2, axis=0, keepdims=True)
-    scale = jnp.broadcast_to(lax.rsqrt(deviation / total + epsilon), (1, BLK))
-    center = jnp.broadcast_to(center, (1, BLK))
+    mean, spread = pltpu.roll(moments, 2 * PART, 1), pltpu.roll(moments, PART, 1)
+    sums = jnp.sum(moments, axis=0, keepdims=True)
+    total = jnp.broadcast_to(sums[:, :1], (1, BLK))
+    center = jnp.broadcast_to(sums[:, PART : PART + 1], (1, BLK)) / total
+    deviation = jnp.sum(spread + moments * (mean - center) ** 2, axis=0, keepdims=True)
+    deviation = jnp.broadcast_to(deviation[:, :1], (1, BLK))
+    scale = lax.rsqrt(deviation / total + epsilon)
     pieces = sems.shape[0]
     depth = moved_ref.shape[0] // pieces
     copies = []
@@ -177,7 +194,7 @@
             pltpu.SMEM((seqs,), i32),
             pltpu.VMEM((seqs, local), f32),
             pltpu.VMEM((seqs, local), f32),
-            pltpu.SemaphoreType.DMA((2 + 2 * (seqs // ROWS),)),
+            pltpu.SemaphoreType.DMA((4,)),
         ],
         compiler_params=params,
         name="advantage",
@@ -187,12 +204,13 @@
         sources.append(lax.ppermute(blocks, "group", [((i + k) % n_group, i) for i in range(n_group)]))
     moments = lax.all_to_all(moments, ("dp", "group"), 0, 0, tiled=True)
     moved, returns = pl.pallas_call(
-        functools.partial(gather_kernel, n_group),
+        functools.partial(gather_kernel, n_group, local // BLK),
         out_shape=(jax.ShapeDtypeStruct((slots, BLK), f32), jax.ShapeDtypeStruct((seqs, local), f32)),
         in_specs=[hbm, vmem] + [vmem] * n_group,
         out_specs=(vmem, hbm),
         scratch_shapes=[
             pltpu.VMEM((n_group * share, BLK), f32),
+            pltpu.VMEM((1, slots), i32),
             pltpu.SMEM((1, slots), i32),
             pltpu.SemaphoreType.DMA((2,)),
         ],

time: 19.7 us -> 19.1 us (0.970)
  waiting for transfers between devices: 5.8 us -> 5.22 us
    pallas_call x1, Pallas kernels: 1.35 us -> 1.92 us  [body(): pl.pallas_call(functools.partial(gather_kernel, n_group, local // BLK), o...]
    all_to_all x1, waiting for transfers between devices: 4.42 us -> 3.85 us  [body(): moments = lax.all_to_all(moments, ('dp', 'group'), 0, 0, tiled=True)]
    pallas_call x1, Pallas kernels: 2.64 us -> 2.24 us  [body(): pl.pallas_call(advantage_kernel, out_shape=(jax.ShapeDtypeStruct((seqs, l...]
    pallas_call x1, Pallas kernels: 1.14 us -> 0.91 us  [body(): pl.pallas_call(whiten_kernel, out_shape=jax.ShapeDtypeStruct((slots, BLK)...]
  transfers between devices with their start and end apart: 2 -> 2, of which waited for: 2 -> 2; matrix products, arithmetic and copies ran while one was open for 0% -> 0% of each run, Pallas kernels for 7% -> 10%
where the time goes in v2:
time: 19.1 us; the launch traced here: 18.9 us
  starting transfers between devices  7.94 us (42%)
  waiting for transfers between devices  5.22 us (27%)
  Pallas kernels  5.07 us (27%)
  between operations  0.66 us (3%)
    all_to_all x1, starting transfers between devices, body(): moments = lax.all_to_all(moments, ('dp', 'group'), 0, 0, tiled=True)  4.92 us
    all_to_all x1, waiting for transfers between devices, body(): moments = lax.all_to_all(moments, ('dp', 'group'), 0, 0, tiled=True)  3.85 us
    ppermute x1, starting transfers between devices, body(): lax.ppermute(blocks, 'group', [((i + k) % n_group, i) for i in range(n_gr...  3.02 us
    pallas_call x1, Pallas kernels, body(): pl.pallas_call(advantage_kernel, out_shape=(jax.ShapeDtypeStruct((seqs, l...  2.24 us
    pallas_call x1, Pallas kernels, body(): pl.pallas_call(functools.partial(gather_kernel, n_group, local // BLK), o...  1.92 us
    ppermute x1, waiting for transfers between devices, body(): lax.ppermute(blocks, 'group', [((i + k) % n_group, i) for i in range(n_gr...  1.38 us
    pallas_call x1, Pallas kernels, body(): pl.pallas_call(whiten_kernel, out_shape=jax.ShapeDtypeStruct((slots, BLK)...  0.91 us
  transfers between devices with their start and end apart: 2, of which 2 were waited for; matrix products, arithmetic and copies ran while one was open for 0% of the time, Pallas kernels for 10%

profile of v2, /device:TPU:0, one launch (start us, length us, event | category | flops | bytes accessed | tf_op | source)
XLA Modules:
  0.0 18.9 jit_solution(2992880859607213669)
XLA Ops:
  0.6 2.2 %advantage.1 = (f32[16,4096]{1,0:T(8,128)S(1)}, f32[512,128]{1,0:T(8,128)S(1)}, f32[32,128]{1,0:T(8,128)}) custom-call(f32[16]{0:T(128)} %horizon_hbm.1, s32[16]{0:T(128)} %lengths_hbm.1, f32[16,4096]{1,0:T(8,128)} %rewards_hbm.1, f32[16,4096]{1,0:T(8,128)} %values_hbm.1), custom_call_target="tpu_custom_call" | custom-call | tf_op jit(solution)/shard_map/advantage/pallas_call | solution.py:183
  2.9 3.0 %collective-permute-start = (f32[512,128]{1,0:T(8,128)S(1)}, f32[512,128]{1,0:T(8,128)S(1)}, u32[]{:S(2)}, u32[]{:S(2)}) collective-permute-start(f32[512,128]{1,0:T(8,128)S(1)} %get-tuple-element.8.refs_0_), channel_id=1, source_target_pairs={{1,0},{0,1},{3,2},{2,3},{5,4},{4,5},{7,6},{6,7},{9,8},{8,9},{11,10... | collective-permute-start | bytes 786440 | tf_op jit(solution)/shard_map/ppermute | solution.py:204
  5.9 4.9 %all-to-all-start = ((f32[32,1,128]{2,1,0:T(1,128)}), f32[32,1,128]{2,1,0:T(1,128)S(1)}, u32[]{:S(2)}, u32[]{:S(2)}) async-start(f32[32,1,128]{2,1,0:T(1,128)} %bitcast.1), calls=%async_computation | async-start | bytes 32768 | tf_op jit(solution)/shard_map/all_to_all | solution.py:205
  10.8 1.4 %collective-permute-done.refs_1_ = f32[512,128]{1,0:T(8,128)S(1)} collective-permute-done((f32[512,128]{1,0:T(8,128)S(1)}, f32[512,128]{1,0:T(8,128)S(1)}, u32[]{:S(2)}, u32[]{:S(2)}) %collective-permute-start) | collective-permute-done | bytes 262176 | tf_op jit(solution)/shard_map/ppermute | solution.py:204
  12.2 1.9 %gather.1 = (f32[512,128]{1,0:T(8,128)S(1)}, f32[16,4096]{1,0:T(8,128)}) custom-call(s32[1,512]{1,0:T(1,128)} %wanted_hbm.1, f32[16,4096]{1,0:T(8,128)S(1)} %get-tuple-element.7.returns_ref, f32[512,128]{1,0:T(8,128)S(1)} %get-tuple-element.8.refs_0_, f32[512,128]{1,0:T(8,128)S(1)} %collective-permute-done.refs_1_), custom_call_target="tpu_custom_call" | custom-call | tf_op jit(solution)/shard_map/gather/pallas_call | solution.py:206
  14.1 3.8 %all-to-all-done = f32[32,1,128]{2,1,0:T(1,128)S(1)} async-done(((f32[32,1,128]{2,1,0:T(1,128)}), f32[32,1,128]{2,1,0:T(1,128)S(1)}, u32[]{:S(2)}, u32[]{:S(2)}) %all-to-all-start) | async-done | bytes 16416 | tf_op jit(solution)/shard_map/all_to_all | solution.py:205
  18.0 0.9 %whiten.1 = f32[512,128]{1,0:T(8,128)} custom-call(f32[32,128]{1,0:T(8,128)S(1)} %bitcast.4, f32[512,128]{1,0:T(8,128)S(1)} %get-tuple-element.11.moved_ref), custom_call_target="tpu_custom_call" | custom-call | tf_op jit(solution)/shard_map/whiten/pallas_call | solution.py:220
Async XLA Ops:
  2.9 9.3 %collective-permute-start = (f32[512,128]{1,0:T(8,128)S(1)}, f32[512,128]{1,0:T(8,128)S(1)}, u32[]{:S(2)}, u32[]{:S(2)}) collective-permute-start(f32[512,128]{1,0:T(8,128)S(1)} %get-tuple-element.8.refs_0_), channel_id=1, source_target_pairs={{1,0},{0,1},{3,2},{2,3},{5,4},{4,5},{7,6},{6,7},{9,8},{8,9},{11,10... | collective-permute-start | bytes 786440 | tf_op jit(solution)/shard_map/ppermute | solution.py:204
  5.9 12.1 %all-to-all-start = ((f32[32,1,128]{2,1,0:T(1,128)}), f32[32,1,128]{2,1,0:T(1,128)S(1)}, u32[]{:S(2)}, u32[]{:S(2)}) async-start(f32[32,1,128]{2,1,0:T(1,128)} %bitcast.1), calls=%async_computation | async-start | bytes 32768 | tf_op jit(solution)/shard_map/all_to_all | solution.py:205
